TPU v7x, 32 devices: a whole 2x2x4 slice. The times are simulated.
32 devices in a mesh: row: 8 (over y, x, core), col: 4 (over z).
Axes of the slice: x: 2, y: 2, z: 4, core: 2. Of those that a mesh axis runs over, the one named last changes fastest.
Arguments:
- species: float32 [4, 64, 32, 256], P(None, None, 'row', 'col'), may hold values from -6 to 6
- symbol_x: float32 [64], replicated, may hold values from 0.3 to 3
- symbol_y: float32 [32], replicated, may hold values from 0.3 to 3
- symbol_z: float32 [256], replicated, may hold values from 0.3 to 3
Outputs:
- coefficients: float32 [4, 64, 32, 256], P(None, 'row', 'col')
All inputs are finite; a program needn't handle non-finite values.
Results may differ from a plain program's by a relative error of at most 0.00007.
Values sent between devices are 32-bit elements; how exact they have to be, the bound alone decides.
A program may use at most 64 MiB of HBM per device.

v0:
```python
import functools

import jax
import jax.numpy as jnp
import ml_dtypes
import numpy as np
from jax import lax
from jax.experimental import pallas as pl
from jax.experimental.pallas import tpu as pltpu
from jax.sharding import PartitionSpec as P

MESH = pl.DeviceIdType.MESH
LANES = 128


def table(count):
    rank = np.arange(count, dtype=np.int64) + 1
    angle = np.pi / (count + 1) * ((rank[:, None] * rank[None, :]) % (2 * count + 2))
    return (np.sin(angle) * (2.0 / (count + 1)) ** 0.5).astype(np.float32)


def halves(values):
    high = values.astype(ml_dtypes.bfloat16)
    low = (values - high.astype(np.float32)).astype(ml_dtypes.bfloat16)
    return np.stack([high, low])


def split(values):
    high = values.astype(jnp.bfloat16)
    low = (values - high.astype(jnp.float32)).astype(jnp.bfloat16)
    return high, low


def side_by_side(values):
    return jnp.concatenate(split(values), axis=-1)


def dot(a, b):
    return jnp.dot(a, b, preferred_element_type=jnp.float32)


def left_dot(both, data):
    count, width = both.shape[0] // 2, data.shape[-1] // 2
    terms = dot(both, data)
    sides = terms[:, :width] + terms[:, width:]
    return sides[:count] + sides[count:]


def far_first(me, slot, count):
    if count != 4:
        return partner(me, count - 1 - slot, count)
    inner = lax.rem((me + 1) // 2, 2)
    outer_to, inner_to = (partner(me, step, count) for step in ((3, 2), (2, 3), (1, 1))[slot])
    return outer_to + (inner_to - outer_to) * inner


def batches(count):
    return [[i] for i in range(count - 2)] + [[count - 2, count - 1]]


def partner(me, step, count):
    if count & (count - 1):
        return lax.rem(me + step, count)
    to, bit = me, 1
    while bit < count:
        if step & bit:
            to = to + bit * (1 - 2 * lax.rem(me // bit, 2))
        bit *= 2
    return to


def kernel(
    dims,
    species, symbol_x, symbol_y, symbol_z, table_x, table_y, table_z,
    out,
    space, mx, my, mz, sx, sy, sz, send_a, recv_a, send_b, recv_b, inverse, held,
    load_sem, store_sem, a_send, a_recv, b_send, b_recv,
):
    fields, pack, rows, cols, cuts, xc, yb, zl = dims
    groups = fields // pack
    row, col = lax.axis_index("row"), lax.axis_index("col")

    pieces = [(species.at[f], space.at[f]) for f in range(fields)]
    pieces += [(table_x.at[q], mx.at[q]) for q in range(cuts)]
    pieces += [(symbol_x, sx), (symbol_y, sy), (symbol_z, sz), (table_y, my), (table_z, mz)]
    loads = [pltpu.make_async_copy(src, dst, load_sem.at[i]) for i, (src, dst) in enumerate(pieces)]
    urgent = list(range(pack)) + [fields]
    for i in urgent:
        loads[i].start()
    row_steps = list(range(rows - 1, 0, -1))
    col_steps = list(range(cols - 1, 0, -1))
    barrier = pltpu.get_barrier_semaphore()
    for step in col_steps:
        pl.semaphore_signal(barrier, inc=1, device_id={"col": partner(col, step, cols)}, device_id_type=MESH)
    for step in row_steps:
        pl.semaphore_signal(barrier, inc=1, device_id={"row": partner(row, step, rows)}, device_id_type=MESH)
    for i in range(fields + cuts):
        if i not in urgent:
            loads[i].start()

    chunks = [(q, g) for g in range(groups) for q in range(cuts)]
    for i, (q, g) in enumerate(chunks):
        if q == 0:
            for k in range(pack):
                loads[g * pack + k].wait()
            data = side_by_side(jnp.concatenate([space[g * pack + k] for k in range(pack)], axis=-1))
        if g == 0:
            loads[fields + q].wait()
        send_a[q, g] = left_dot(mx[q], data).reshape(send_a.shape[2:])
        if i == 0:
            for load in loads[fields + cuts:]:
                load.start()
            pl.semaphore_wait(barrier, len(row_steps) + len(col_steps))
        for step in row_steps:
            to = partner(row, step, rows)
            pltpu.make_async_remote_copy(
                src_ref=send_a.at[q, g, to], dst_ref=recv_a.at[q, g, row],
                send_sem=a_send, recv_sem=a_recv.at[i],
                device_id={"row": to}, device_id_type=MESH,
            ).start()
        recv_a[q, g, row] = send_a[q, g, row]

    for load in loads[fields + cuts:]:
        load.wait()
    part_y = jnp.zeros((yb, 1), jnp.float32)
    at = lax.broadcasted_iota(jnp.int32, (yb, 1), 0)
    for j in range(yb):
        part_y = jnp.where(at == j, sy[col * yb + j], part_y)
    for i in range(cuts * xc):
        inverse[i] = 1.0 / ((sx[row * (cuts * xc) + i] + part_y) + sz[...])

    def pass_on(i, slot):
        q, g = chunks[i]
        to = far_first(col, slot, cols)
        pltpu.make_async_remote_copy(
            src_ref=send_b.at[q, g, to], dst_ref=recv_b.at[q, g, col],
            send_sem=b_send, recv_sem=b_recv.at[i],
            device_id={"col": to}, device_id_type=MESH,
        ).start()

    for i, (q, g) in enumerate(chunks):
        arrived = recv_a.at[q, g, pl.ds(0, rows - 1)]
        pltpu.make_async_copy(arrived, arrived, a_recv.at[i]).wait()
        lines = recv_a[q, g].reshape(-1, LANES)
        send_b[q, g] = left_dot(my[...], side_by_side(lines)).reshape(send_b.shape[2:])
        for slot in range(1):
            pass_on(i, slot)
        recv_b[q, g, col] = send_b[q, g, col]

    for i, slot in [(i, s) for s in range(1, cols - 1) for i in range(len(chunks)) ]:
        pass_on(i, slot)
    stores = []
    height = xc * yb
    for batch in batches(len(chunks)):
        lines = []
        for i in batch:
            q, g = chunks[i]
            arrived = recv_b.at[q, g, pl.ds(0, cols - 1)]
            pltpu.make_async_copy(arrived, arrived, b_recv.at[i]).wait()
            blocks = [recv_b[q, g, c] for c in range(cols)]
            for k in range(pack):
                lines.append(jnp.concatenate([b[:, k * zl:(k + 1) * zl] for b in blocks], axis=-1))
        high, low = split(jnp.concatenate(lines, axis=0))
        most = dot(jnp.concatenate([high, low], axis=0), mz[0])
        count = high.shape[0]
        result = most[:count] + most[count:] + dot(high, mz[1])
        for n, i in enumerate(batch):
            q, g = chunks[i]
            factor = inverse[q * xc:(q + 1) * xc].reshape(height, -1)
            for k in range(pack):
                at_line = (n * pack + k) * height
                held[i, k] = result[at_line:at_line + height] * factor
            stores.append(pltpu.make_async_copy(
                held.at[i], out.at[pl.ds(g * pack, pack), pl.ds(q * height, height)], store_sem.at[i]
            ))
            stores[-1].start()

    sent = send_a.at[:, :, pl.ds(0, rows - 1)]
    pltpu.make_async_copy(sent, sent, a_send).wait()
    sent = send_b.at[:, :, pl.ds(0, cols - 1)]
    pltpu.make_async_copy(sent, sent, b_send).wait()
    for store in stores:
        store.wait()


def on_device(rows, cols, species, symbol_x, symbol_y, symbol_z):
    fields, x, yl, zl = species.shape
    y, z = symbol_y.shape[0], symbol_z.shape[0]
    xb, yb = x // rows, y // cols
    pack = LANES // zl
    groups = fields // pack
    cuts = 2
    xc = xb // cuts

    hx = table(x)
    eye = np.eye(yl, dtype=np.float32)
    full_x = np.einsum("rqia,yb->qriyab", hx.T.reshape(rows, cuts, xc, x), eye).reshape(cuts, rows * xc * yl, x * yl)
    hy = table(y).T.reshape(cols, yb, rows, yl)
    full_y = np.einsum("cmry,ij->cimrjy", hy, np.eye(xc, dtype=np.float32)).reshape(cols * xc * yb, rows * xc * yl)
    tables = [
        np.concatenate(list(halves(full_x)), axis=1), np.concatenate(list(halves(full_y)), axis=0), halves(table(z))
    ]

    any_space = pl.BlockSpec(memory_space=pltpu.MemorySpace.HBM)
    chunks = cuts * groups
    a_shape = (cuts, groups, rows, xc * yl, LANES)
    b_shape = (cuts, groups, cols, xc * yb, LANES)
    dma = pltpu.SemaphoreType.DMA
    out = pl.pallas_call(
        functools.partial(kernel, (fields, pack, rows, cols, cuts, xc, yb, zl)),
        out_shape=pltpu.MemorySpace.VMEM((fields, xb * yb, z), jnp.float32),
        in_specs=[any_space] * 7,
        out_specs=pl.BlockSpec(memory_space=pl.ANY),
        scratch_shapes=[
            pltpu.VMEM((fields, x * yl, zl), jnp.float32),
            pltpu.VMEM(tables[0].shape, jnp.bfloat16),
            pltpu.VMEM(tables[1].shape, jnp.bfloat16),
            pltpu.VMEM(tables[2].shape, jnp.bfloat16),
            pltpu.SMEM((x,), jnp.float32),
            pltpu.SMEM((y,), jnp.float32),
            pltpu.VMEM((1, z), jnp.float32),
            pltpu.VMEM(a_shape, jnp.float32),
            pltpu.VMEM(a_shape, jnp.float32),
            pltpu.VMEM(b_shape, jnp.float32),
            pltpu.VMEM(b_shape, jnp.float32),
            pltpu.VMEM((xb, yb, z), jnp.float32),
            pltpu.VMEM((chunks, pack, xc * yb, z), jnp.float32),
            dma((fields + cuts + 5,)),
            dma((chunks,)),
            dma,
            dma((chunks,)),
            dma,
            dma((chunks,)),
        ],
        compiler_params=pltpu.CompilerParams(
            collective_id=0, has_side_effects=True, vmem_limit_bytes=60 * 1024 * 1024
        ),
    )(
        species.reshape(fields, x * yl, zl), symbol_x, symbol_y, symbol_z.reshape(1, z),
        *[jnp.asarray(t) for t in tables],
    )
    return out.reshape(fields, xb, yb, z)


def solution(mesh):
    placed = (P(None, None, "row", "col"), P(), P(), P())
    return jax.shard_map(
        functools.partial(on_device, mesh.shape["row"], mesh.shape["col"]),
        mesh=mesh,
        in_specs=placed,
        out_specs=P(None, "row", "col", None),
        check_vma=False,
    )
```

profile of v0, /device:TPU:0, one launch (start us, length us, event | category | flops | bytes accessed | tf_op | source)
XLA Modules:
  0.0 17.2 jit_solution(14539923154672672282)
XLA Ops:
  0.0 16.4 %shard_map.73 = f32[4,64,256]{2,1,0:T(8,128)S(1)} custom-call(f32[4,256,64]{2,1,0:T(8,128)} %bitcast.4, f32[64]{0:T(128)} %symbol_x.1, f32[32]{0:T(128)} %symbol_y.1, f32[1,256]{1,0:T(1,128)} %bitcast.5, bf16[2,256,256]{2,1,0:T(8,128)(2,1)} %constant.6.clone.table_x, bf16[256,128]{1,0:T(8,128)(2,1)} %constant.7.clone.table_y, ...), custom_call_target="tpu_custom_call" | custom-call | tf_op jit(solution)/shard_map/pallas_call | solution.py:209
  16.4 0.7 %copy.9 = f32[4,8,8,256]{3,2,1,0:T(8,128)} copy(f32[4,8,8,256]{3,2,1,0:T(8,128)S(1)} %bitcast.3) | data formatting | bytes 524288
where the time goes:
time: 17.3 us; the launch traced here: 17.2 us
  Pallas kernels  16.4 us (95%)
  local copies, waits for them, and re-layouts  0.71 us (4%)
    pallas_call x1, Pallas kernels, on_device(): pl.pallas_call(functools.partial(kernel, (fields, pack, rows, cols, cuts,...  16.4 us
    unnamed x1, local copies, waits for them, and re-layouts  0.71 us

commit v1 on v0

v1 whole, which is shorter than its diff:
```python
import functools

import jax
import jax.numpy as jnp
import ml_dtypes
import numpy as np
from jax import lax
from jax.experimental import pallas as pl
from jax.experimental.pallas import tpu as pltpu
from jax.sharding import PartitionSpec as P

MESH = pl.DeviceIdType.MESH
LANES = 128
SUBLANES = 8


def table(count):
    rank = np.arange(count, dtype=np.int64) + 1
    angle = np.pi / (count + 1) * ((rank[:, None] * rank[None, :]) % (2 * count + 2))
    return (np.sin(angle) * (2.0 / (count + 1)) ** 0.5).astype(np.float32)


def halves(values):
    high = values.astype(ml_dtypes.bfloat16)
    low = (values - high.astype(np.float32)).astype(ml_dtypes.bfloat16)
    return np.stack([high, low])


def split(values):
    high = values.astype(jnp.bfloat16)
    low = (values - high.astype(jnp.float32)).astype(jnp.bfloat16)
    return high, low


def side_by_side(values):
    return jnp.concatenate(split(values), axis=-1)


def dot(a, b):
    return jnp.dot(a, b, preferred_element_type=jnp.float32)


def left_dot(both, data):
    count, width = both.shape[0] // 2, data.shape[-1] // 2
    terms = dot(both, data)
    sides = terms[:, :width] + terms[:, width:]
    return sides[:count] + sides[count:]


def partner(me, step, count):
    if count & (count - 1):
        return lax.rem(me + step, count)
    to, bit = me, 1
    while bit < count:
        if step & bit:
            to = to + bit * (1 - 2 * lax.rem(me // bit, 2))
        bit *= 2
    return to


def chunk_list(cuts, groups):
    if cuts == 4 and groups == 2:
        return [(0, 0, 1), (0, 1, 1), (0, 2, 2), (1, 0, 2), (1, 2, 2)]
    return [(g, q, 1) for g in range(groups) for q in range(cuts)]


def batch_list(count):
    return [[0, 1], [2], [3], [4]]


ORDERS = (
    (3, 2, 1), (0, 3, 2), (3, 0, 1), (0, 1, 2),
    (3, 2, 1), (0, 3, 2), (3, 0, 1), (0, 1, 2),
    (3, 2, 1), (0, 3, 2), (3, 0, 1), (0, 1, 2),
    (3, 2, 1), (0, 3, 2), (3, 0, 1), (0, 1, 2),
)
EARLY = (
    (1, 0, 0), (1, 1, 0), (1, 1, 0), (1, 0, 0),
    (1, 0, 0), (1, 1, 0), (1, 1, 0), (0, 0, 0),
    (1, 0, 0), (1, 1, 0), (1, 1, 0), (1, 0, 0),
    (1, 0, 0), (1, 1, 0), (1, 1, 0), (1, 0, 0),
)


def pick(at, values):
    return sum(value * jnp.maximum(0, 1 - abs(at - i)) for i, value in enumerate(values) if value)


def passes(row, col, count):
    if count != 4:
        return [(partner(col, count - 1 - slot, count), 1 - min(slot, 1)) for slot in range(count - 1)]
    small = jnp.minimum(row, 2)
    at = count * (small + lax.div(small, 2) * lax.rem(row, 2)) + col
    return [(pick(at, [o[s] for o in ORDERS]), pick(at, [e[s] for e in EARLY])) for s in range(count - 1)]


def kernel(
    dims,
    species, symbol_x, symbol_y, symbol_z, table_x, table_y, table_z,
    out,
    space, mx, my, mz, sx, sy, sz, send_a, recv_a, send_b, recv_b, inverse,
    a_send, a_recv, b_send, b_recv, ready,
):
    fields, pack, rows, cols, cuts, xc, yb, zl = dims
    groups = fields // pack
    row, col = lax.axis_index("row"), lax.axis_index("col")
    chunks = chunk_list(cuts, groups)

    row_steps = list(range(rows - 1, 0, -1))
    col_steps = list(range(cols - 1, 0, -1))
    barrier = pltpu.get_barrier_semaphore()
    odd = lax.rem(row, 2)
    twin = row + 1 - 2 * odd

    def first_part(load_sem):
        pieces = [(species.at[f], space.at[f]) for f in range(fields)]
        pieces += [(table_x.at[q], mx.at[q]) for q in range(cuts)]
        pieces += [(symbol_x, sx), (symbol_y, sy), (symbol_z, sz), (table_y, my), (table_z, mz)]
        loads = [pltpu.make_async_copy(src, dst, load_sem.at[i]) for i, (src, dst) in enumerate(pieces)]
        urgent = list(range(pack)) + [fields]
        for i in urgent:
            loads[i].start()
        for pair in range(rows // 2):
            @pl.when(row != 2 * pair + 1)
            def _():
                pl.semaphore_signal(barrier, inc=1, device_id={"row": 2 * pair + 1}, device_id_type=MESH)
        for step in col_steps:
            to = {"row": row - odd, "col": partner(col, step, cols)}
            pl.semaphore_signal(barrier, inc=1, device_id=to, device_id_type=MESH)

        @pl.when(odd == 1)
        def _():
            pl.semaphore_signal(barrier, inc=1, device_id={"row": twin}, device_id_type=MESH)

        for i in range(fields + cuts):
            if i not in urgent:
                loads[i].start()

        for i, (g, q, n) in enumerate(chunks):
            if q == 0:
                for k in range(pack):
                    loads[g * pack + k].wait()
                data = side_by_side(jnp.concatenate([space[g * pack + k] for k in range(pack)], axis=-1))
            if g == 0:
                for p in range(q, q + n):
                    loads[fields + p].wait()
            for p in range(q, q + n):
                send_a[g, :, p] = left_dot(mx[p], data).reshape(rows, -1, LANES)
            if i == 0:

                @pl.when(odd == 1)
                def _():
                    pl.semaphore_wait(barrier, len(row_steps))
                    pl.semaphore_signal(ready, inc=1, device_id={"row": twin}, device_id_type=MESH)

                @pl.when(odd == 0)
                def _():
                    pl.semaphore_wait(ready, 1)

            for even_step, odd_step in zip(row_steps[1::2] + row_steps[::2], row_steps[::2] + row_steps[1::2]):
                to = partner(row, even_step, rows)
                to = to + (partner(row, odd_step, rows) - to) * odd
                pltpu.make_async_remote_copy(
                    src_ref=send_a.at[g, to, pl.ds(q, n)], dst_ref=recv_a.at[g, row, pl.ds(q, n)],
                    send_sem=a_send, recv_sem=a_recv.at[i],
                    device_id={"row": to}, device_id_type=MESH,
                ).start()
            recv_a[g, row, pl.ds(q, n)] = send_a[g, row, pl.ds(q, n)]
            if i == 0:
                for load in loads[fields + cuts:]:
                    load.start()

        for load in loads[fields + cuts:]:
            load.wait()
        part_y = jnp.zeros((yb, 1), jnp.float32)
        at = lax.broadcasted_iota(jnp.int32, (yb, 1), 0)
        for j in range(yb):
            part_y = jnp.where(at == j, sy[col * yb + j], part_y)
        for i in range(cuts * xc):
            inverse[i] = 1.0 / ((sx[row * (cuts * xc) + i] + part_y) + sz[...])

    pl.run_scoped(first_part, pltpu.SemaphoreType.DMA((fields + cuts + 5,)))

    @pl.when(odd == 0)
    def _():
        pl.semaphore_wait(barrier, 2 * len(col_steps) + 1)
        pl.semaphore_signal(ready, inc=1, device_id={"row": twin}, device_id_type=MESH)

    @pl.when(odd == 1)
    def _():
        pl.semaphore_wait(ready, 1)

    batches = batch_list(len(chunks))
    hops = passes(row, col, cols)

    def batch_of(i):
        return [i in batch for batch in batches].index(True)

    def pass_on(i, slot):
        g, q, n = chunks[i]
        to = hops[slot][0]
        pltpu.make_async_remote_copy(
            src_ref=send_b.at[g, to, pl.ds(q, n)], dst_ref=recv_b.at[g, col, pl.ds(q, n)],
            send_sem=b_send, recv_sem=b_recv.at[batch_of(i)],
            device_id={"col": to}, device_id_type=MESH,
        ).start()

    for i, (g, q, n) in enumerate(chunks):
        arrived = recv_a.at[g, pl.ds(0, rows - 1), pl.ds(q, n)]
        pltpu.make_async_copy(arrived, arrived, a_recv.at[i]).wait()
        for p in range(q, q + n):
            lines = recv_a[g, :, p].reshape(-1, LANES)
            send_b[g, :, p] = left_dot(my[...], side_by_side(lines)).reshape(cols, -1, LANES)
        for slot in range(cols - 1):
            pl.when(hops[slot][1] == 1)(functools.partial(pass_on, i, slot))
        recv_b[g, col, pl.ds(q, n)] = send_b[g, col, pl.ds(q, n)]
    for slot in range(cols - 1):
        for i in range(len(chunks)):
            pl.when(hops[slot][1] == 0)(functools.partial(pass_on, i, slot))

    height = xc * yb
    for batch in batches:
        lines = []
        g, q, n = chunks[batch[0]]
        arrived = recv_b.at[g, pl.ds(0, cols - 1), pl.ds(q, sum(chunks[i][2] for i in batch))]
        pltpu.make_async_copy(arrived, arrived, b_recv.at[batch_of(batch[0])]).wait()
        for i in batch:
            g, q, n = chunks[i]
            for p in range(q, q + n):
                blocks = [recv_b[g, c, p] for c in range(cols)]
                for k in range(pack):
                    lines.append(jnp.concatenate([b[:, k * zl:(k + 1) * zl] for b in blocks], axis=-1))
        high, low = split(jnp.concatenate(lines, axis=0))
        most = dot(jnp.concatenate([high, low], axis=0), mz[0])
        count = high.shape[0]
        result = most[:count] + most[count:] + dot(high, mz[1])
        at_line = 0
        for i in batch:
            g, q, n = chunks[i]
            for p in range(q, q + n):
                factor = inverse[p * xc:(p + 1) * xc].reshape(height, -1)
                for k in range(pack):
                    out[g * pack + k, pl.ds(p * height, height)] = result[at_line:at_line + height] * factor
                    at_line += height

    sent = send_a.at[:, pl.ds(0, rows - 1)]
    pltpu.make_async_copy(sent, sent, a_send).wait()
    sent = send_b.at[:, pl.ds(0, cols - 1)]
    pltpu.make_async_copy(sent, sent, b_send).wait()


def on_device(rows, cols, species, symbol_x, symbol_y, symbol_z):
    fields, x, yl, zl = species.shape
    y, z = symbol_y.shape[0], symbol_z.shape[0]
    xb, yb = x // rows, y // cols
    pack = LANES // zl
    groups = fields // pack
    xc = max(1, SUBLANES // yl)
    cuts = xb // xc

    hx = table(x)
    eye = np.eye(yl, dtype=np.float32)
    full_x = np.einsum("rqia,yb->qriyab", hx.T.reshape(rows, cuts, xc, x), eye).reshape(cuts, rows * xc * yl, x * yl)
    hy = table(y).T.reshape(cols, yb, rows, yl)
    full_y = np.einsum("cmry,ij->cimrjy", hy, np.eye(xc, dtype=np.float32)).reshape(cols * xc * yb, rows * xc * yl)
    tables = [
        np.concatenate(list(halves(full_x)), axis=1), np.concatenate(list(halves(full_y)), axis=0), halves(table(z))
    ]

    any_space = pl.BlockSpec(memory_space=pltpu.MemorySpace.HBM)
    chunks = len(chunk_list(cuts, groups))
    a_shape = (groups, rows, cuts, xc * yl, LANES)
    b_shape = (groups, cols, cuts, xc * yb, LANES)
    dma = pltpu.SemaphoreType.DMA
    out = pl.pallas_call(
        functools.partial(kernel, (fields, pack, rows, cols, cuts, xc, yb, zl)),
        out_shape=pltpu.MemorySpace.VMEM((fields, xb * yb, z), jnp.float32),
        in_specs=[any_space] * 7,
        out_specs=pl.BlockSpec(memory_space=pltpu.MemorySpace.VMEM),
        scratch_shapes=[
            pltpu.VMEM((fields, x * yl, zl), jnp.float32),
            pltpu.VMEM(tables[0].shape, jnp.bfloat16),
            pltpu.VMEM(tables[1].shape, jnp.bfloat16),
            pltpu.VMEM(tables[2].shape, jnp.bfloat16),
            pltpu.SMEM((x,), jnp.float32),
            pltpu.SMEM((y,), jnp.float32),
            pltpu.VMEM((1, z), jnp.float32),
            pltpu.VMEM(a_shape, jnp.float32),
            pltpu.VMEM(a_shape, jnp.float32),
            pltpu.VMEM(b_shape, jnp.float32),
            pltpu.VMEM(b_shape, jnp.float32),
            pltpu.VMEM((xb, yb, z), jnp.float32),
            dma,
            dma((chunks,)),
            dma,
            dma((len(batch_list(chunks)),)),
            pltpu.SemaphoreType.REGULAR,
        ],
        compiler_params=pltpu.CompilerParams(
            collective_id=0, has_side_effects=True, vmem_limit_bytes=60 * 1024 * 1024
        ),
    )(
        species.reshape(fields, x * yl, zl), symbol_x, symbol_y, symbol_z.reshape(1, z),
        *[jnp.asarray(t) for t in tables],
    )
    return out.reshape(fields, xb, yb, z)


def solution(mesh):
    placed = (P(None, None, "row", "col"), P(), P(), P())
    return jax.shard_map(
        functools.partial(on_device, mesh.shape["row"], mesh.shape["col"]),
        mesh=mesh,
        in_specs=placed,
        out_specs=P(None, "row", "col", None),
        check_vma=False,
    )
```

time: 17.3 us -> 15.8 us (0.913)
  the two profiles are of different devices: /device:TPU:0 before, /device:TPU:8 now
where the time goes in v1:
time: 15.8 us; the launch traced here: 15.6 us
  Pallas kernels  14.9 us (94%)
  local copies, waits for them, and re-layouts  0.71 us (4%)
    pallas_call x1, Pallas kernels, on_device(): pl.pallas_call(functools.partial(kernel, (fields, pack, rows, cols, cuts,...  14.9 us
    unnamed x1, local copies, waits for them, and re-layouts  0.71 us

profile of v1, /device:TPU:8, one launch (start us, length us, event | category | flops | bytes accessed | tf_op | source)
XLA Modules:
  0.0 15.6 jit_solution(13517510047619491863)
XLA Ops:
  0.0 14.9 %shard_map.73 = f32[4,64,256]{2,1,0:T(8,128)S(1)} custom-call(f32[4,256,64]{2,1,0:T(8,128)} %bitcast.4, f32[64]{0:T(128)} %symbol_x.1, f32[32]{0:T(128)} %symbol_y.1, f32[1,256]{1,0:T(1,128)} %bitcast.5, bf16[4,128,256]{2,1,0:T(8,128)(2,1)} %constant.6.clone.table_x, bf16[128,64]{1,0:T(8,128)(2,1)} %constant.7.clone.table_y, ...), custom_call_target="tpu_custom_call" | custom-call | tf_op jit(solution)/shard_map/pallas_call | solution.py:275
  14.9 0.7 %copy.9 = f32[4,8,8,256]{3,2,1,0:T(8,128)} copy(f32[4,8,8,256]{3,2,1,0:T(8,128)S(1)} %bitcast.3) | data formatting | bytes 524288

commit v2 on v1

--- a/solution.py
+++ b/solution.py
@@ -65,20 +65,20 @@
 
 
 def batch_list(count):
-    return [[0, 1], [2], [3], [4]]
+    return [[0, 1], [2], [3], [4]] if count == 5 else [[i] for i in range(count)]
 
 
 ORDERS = (
     (3, 2, 1), (0, 3, 2), (3, 0, 1), (0, 1, 2),
     (3, 2, 1), (0, 3, 2), (3, 0, 1), (0, 1, 2),
     (3, 2, 1), (0, 3, 2), (3, 0, 1), (0, 1, 2),
-    (3, 2, 1), (0, 3, 2), (3, 0, 1), (0, 1, 2),
+    (3, 2, 1), (0, 3, 2), (3, 0, 1), (0, 2, 1),
 )
 EARLY = (
     (1, 0, 0), (1, 1, 0), (1, 1, 0), (1, 0, 0),
-    (1, 0, 0), (1, 1, 0), (1, 1, 0), (0, 0, 0),
+    (1, 0, 0), (1, 1, 0), (1, 1, 1), (0, 0, 0),
     (1, 0, 0), (1, 1, 0), (1, 1, 0), (1, 0, 0),
-    (1, 0, 0), (1, 1, 0), (1, 1, 0), (1, 0, 0),
+    (1, 0, 0), (1, 1, 0), (1, 1, 1), (1, 0, 0),
 )
 
 

time: 15.8 us -> 15.5 us (0.981)
  the two profiles are of different devices: /device:TPU:8 before, /device:TPU:0 now
where the time goes in v2:
time: 15.5 us; the launch traced here: 15.3 us
  Pallas kernels  14.6 us (94%)
  local copies, waits for them, and re-layouts  0.71 us (5%)
    pallas_call x1, Pallas kernels, on_device(): pl.pallas_call(functools.partial(kernel, (fields, pack, rows, cols, cuts,...  14.6 us
    unnamed x1, local copies, waits for them, and re-layouts  0.71 us

profile of v2, /device:TPU:0, one launch (start us, length us, event | category | flops | bytes accessed | tf_op | source)
XLA Modules:
  0.0 15.3 jit_solution(1351318549909790636)
XLA Ops:
  0.0 14.6 %shard_map.73 = f32[4,64,256]{2,1,0:T(8,128)S(1)} custom-call(f32[4,256,64]{2,1,0:T(8,128)} %bitcast.4, f32[64]{0:T(128)} %symbol_x.1, f32[32]{0:T(128)} %symbol_y.1, f32[1,256]{1,0:T(1,128)} %bitcast.5, bf16[4,128,256]{2,1,0:T(8,128)(2,1)} %constant.6.clone.table_x, bf16[128,64]{1,0:T(8,128)(2,1)} %constant.7.clone.table_y, ...), custom_call_target="tpu_custom_call" | custom-call | tf_op jit(solution)/shard_map/pallas_call | solution.py:275
  14.6 0.7 %copy.9 = f32[4,8,8,256]{3,2,1,0:T(8,128)} copy(f32[4,8,8,256]{3,2,1,0:T(8,128)S(1)} %bitcast.3) | data formatting | bytes 524288

commit v3 on v2

--- a/solution.py
+++ b/solution.py
@@ -11,6 +11,7 @@
 
 MESH = pl.DeviceIdType.MESH
 LANES = 128
+PIECES = 4
 SUBLANES = 8
 
 
@@ -99,7 +100,7 @@
     species, symbol_x, symbol_y, symbol_z, table_x, table_y, table_z,
     out,
     space, mx, my, mz, sx, sy, sz, send_a, recv_a, send_b, recv_b, inverse,
-    a_send, a_recv, b_send, b_recv, ready,
+    b_send, b_recv, ready,
 ):
     fields, pack, rows, cols, cuts, xc, yb, zl = dims
     groups = fields // pack
@@ -112,14 +113,25 @@
     odd = lax.rem(row, 2)
     twin = row + 1 - 2 * odd
 
-    def first_part(load_sem):
+    batches = batch_list(len(chunks))
+
+    def batch_of(i):
+        return [i in batch for batch in batches].index(True)
+
+    def first_part(load_sem, a_send, a_recv):
         pieces = [(species.at[f], space.at[f]) for f in range(fields)]
         pieces += [(table_x.at[q], mx.at[q]) for q in range(cuts)]
         pieces += [(symbol_x, sx), (symbol_y, sy), (symbol_z, sz), (table_y, my), (table_z, mz)]
-        loads = [pltpu.make_async_copy(src, dst, load_sem.at[i]) for i, (src, dst) in enumerate(pieces)]
-        urgent = list(range(pack)) + [fields]
-        for i in urgent:
-            loads[i].start()
+        loads = [
+            None if i < pack else pltpu.make_async_copy(src, dst, load_sem.at[i])
+            for i, (src, dst) in enumerate(pieces)
+        ]
+        loads[fields].start()
+        height = space.shape[1] // PIECES
+        for i in range(PIECES):
+            for f in range(pack):
+                part = pl.ds(i * height, height)
+                pltpu.make_async_copy(species.at[f, part], space.at[f, part], load_sem.at[0]).start()
         for pair in range(rows // 2):
             @pl.when(row != 2 * pair + 1)
             def _():
@@ -132,17 +144,23 @@
         def _():
             pl.semaphore_signal(barrier, inc=1, device_id={"row": twin}, device_id_type=MESH)
 
-        for i in range(fields + cuts):
-            if i not in urgent:
-                loads[i].start()
+        for load in loads[fields + 1:fields + cuts]:
+            load.start()
 
         for i, (g, q, n) in enumerate(chunks):
             if q == 0:
-                for k in range(pack):
-                    loads[g * pack + k].wait()
+                if g == 0:
+                    loads[fields].wait()
+                    for load in loads[pack:fields]:
+                        load.start()
+                    group = space.at[pl.ds(0, pack)]
+                    pltpu.make_async_copy(group, group, load_sem.at[0]).wait()
+                else:
+                    for k in range(pack):
+                        loads[g * pack + k].wait()
                 data = side_by_side(jnp.concatenate([space[g * pack + k] for k in range(pack)], axis=-1))
             if g == 0:
-                for p in range(q, q + n):
+                for p in range(max(q, 1), q + n):
                     loads[fields + p].wait()
             for p in range(q, q + n):
                 send_a[g, :, p] = left_dot(mx[p], data).reshape(rows, -1, LANES)
@@ -179,44 +197,45 @@
         for i in range(cuts * xc):
             inverse[i] = 1.0 / ((sx[row * (cuts * xc) + i] + part_y) + sz[...])
 
-    pl.run_scoped(first_part, pltpu.SemaphoreType.DMA((fields + cuts + 5,)))
-
-    @pl.when(odd == 0)
-    def _():
-        pl.semaphore_wait(barrier, 2 * len(col_steps) + 1)
-        pl.semaphore_signal(ready, inc=1, device_id={"row": twin}, device_id_type=MESH)
-
-    @pl.when(odd == 1)
-    def _():
-        pl.semaphore_wait(ready, 1)
-
-    batches = batch_list(len(chunks))
-    hops = passes(row, col, cols)
-
-    def batch_of(i):
-        return [i in batch for batch in batches].index(True)
-
-    def pass_on(i, slot):
-        g, q, n = chunks[i]
-        to = hops[slot][0]
-        pltpu.make_async_remote_copy(
-            src_ref=send_b.at[g, to, pl.ds(q, n)], dst_ref=recv_b.at[g, col, pl.ds(q, n)],
-            send_sem=b_send, recv_sem=b_recv.at[batch_of(i)],
-            device_id={"col": to}, device_id_type=MESH,
-        ).start()
-
-    for i, (g, q, n) in enumerate(chunks):
-        arrived = recv_a.at[g, pl.ds(0, rows - 1), pl.ds(q, n)]
-        pltpu.make_async_copy(arrived, arrived, a_recv.at[i]).wait()
-        for p in range(q, q + n):
-            lines = recv_a[g, :, p].reshape(-1, LANES)
-            send_b[g, :, p] = left_dot(my[...], side_by_side(lines)).reshape(cols, -1, LANES)
+
+        @pl.when(odd == 0)
+        def _():
+            pl.semaphore_wait(barrier, 2 * len(col_steps) + 1)
+            pl.semaphore_signal(ready, inc=1, device_id={"row": twin}, device_id_type=MESH)
+
+        @pl.when(odd == 1)
+        def _():
+            pl.semaphore_wait(ready, 1)
+
+        hops = passes(row, col, cols)
+
+        def pass_on(i, slot):
+            g, q, n = chunks[i]
+            to = hops[slot][0]
+            pltpu.make_async_remote_copy(
+                src_ref=send_b.at[g, to, pl.ds(q, n)], dst_ref=recv_b.at[g, col, pl.ds(q, n)],
+                send_sem=b_send, recv_sem=b_recv.at[batch_of(i)],
+                device_id={"col": to}, device_id_type=MESH,
+            ).start()
+
+        for i, (g, q, n) in enumerate(chunks):
+            arrived = recv_a.at[g, pl.ds(0, rows - 1), pl.ds(q, n)]
+            pltpu.make_async_copy(arrived, arrived, a_recv.at[i]).wait()
+            for p in range(q, q + n):
+                lines = recv_a[g, :, p].reshape(-1, LANES)
+                send_b[g, :, p] = left_dot(my[...], side_by_side(lines)).reshape(cols, -1, LANES)
+            for slot in range(cols - 1):
+                pl.when(hops[slot][1] == 1)(functools.partial(pass_on, i, slot))
+            recv_b[g, col, pl.ds(q, n)] = send_b[g, col, pl.ds(q, n)]
         for slot in range(cols - 1):
-            pl.when(hops[slot][1] == 1)(functools.partial(pass_on, i, slot))
-        recv_b[g, col, pl.ds(q, n)] = send_b[g, col, pl.ds(q, n)]
-    for slot in range(cols - 1):
-        for i in range(len(chunks)):
-            pl.when(hops[slot][1] == 0)(functools.partial(pass_on, i, slot))
+            for i in range(len(chunks)):
+                pl.when(hops[slot][1] == 0)(functools.partial(pass_on, i, slot))
+
+        sent = send_a.at[:, pl.ds(0, rows - 1)]
+        pltpu.make_async_copy(sent, sent, a_send).wait()
+
+    dma = pltpu.SemaphoreType.DMA
+    pl.run_scoped(first_part, dma((fields + cuts + 5,)), dma, dma((len(chunks),)))
 
     height = xc * yb
     for batch in batches:
@@ -243,8 +262,6 @@
                     out[g * pack + k, pl.ds(p * height, height)] = result[at_line:at_line + height] * factor
                     at_line += height
 
-    sent = send_a.at[:, pl.ds(0, rows - 1)]
-    pltpu.make_async_copy(sent, sent, a_send).wait()
     sent = send_b.at[:, pl.ds(0, cols - 1)]
     pltpu.make_async_copy(sent, sent, b_send).wait()
 
@@ -291,8 +308,6 @@
             pltpu.VMEM(b_shape, jnp.float32),
             pltpu.VMEM((xb, yb, z), jnp.float32),
             dma,
-            dma((chunks,)),
-            dma,
             dma((len(batch_list(chunks)),)),
             pltpu.SemaphoreType.REGULAR,
         ],

time: 15.5 us -> 15.4 us (level)
  no operation moved by 1% of the time
where the time goes in v3:
time: 15.4 us; the launch traced here: 15.2 us
  Pallas kernels  14.5 us (94%)
  local copies, waits for them, and re-layouts  0.71 us (5%)
    pallas_call x1, Pallas kernels, on_device(): pl.pallas_call(functools.partial(kernel, (fields, pack, rows, cols, cuts,...  14.5 us
    unnamed x1, local copies, waits for them, and re-layouts  0.71 us

profile of v3, /device:TPU:0, one launch (start us, length us, event | category | flops | bytes accessed | tf_op | source)
XLA Modules:
  0.0 15.2 jit_solution(3403432678609979000)
XLA Ops:
  0.0 14.5 %shard_map.73 = f32[4,64,256]{2,1,0:T(8,128)S(1)} custom-call(f32[4,256,64]{2,1,0:T(8,128)} %bitcast.4, f32[64]{0:T(128)} %symbol_x.1, f32[32]{0:T(128)} %symbol_y.1, f32[1,256]{1,0:T(1,128)} %bitcast.5, bf16[4,128,256]{2,1,0:T(8,128)(2,1)} %constant.6.clone.table_x, bf16[128,64]{1,0:T(8,128)(2,1)} %constant.7.clone.table_y, ...), custom_call_target="tpu_custom_call" | custom-call | tf_op jit(solution)/shard_map/pallas_call | solution.py:292
  14.5 0.7 %copy.9 = f32[4,8,8,256]{3,2,1,0:T(8,128)} copy(f32[4,8,8,256]{3,2,1,0:T(8,128)S(1)} %bitcast.3) | data formatting | bytes 524288

commit v4 on v3

--- a/solution.py
+++ b/solution.py
@@ -11,7 +11,7 @@
 
 MESH = pl.DeviceIdType.MESH
 LANES = 128
-PIECES = 4
+PIECES = 8
 SUBLANES = 8
 
 
@@ -66,7 +66,7 @@
 
 
 def batch_list(count):
-    return [[0, 1], [2], [3], [4]] if count == 5 else [[i] for i in range(count)]
+    return [[0, 1, 2], [3], [4]] if count == 5 else [[i] for i in range(count)]
 
 
 ORDERS = (
@@ -100,7 +100,7 @@
     species, symbol_x, symbol_y, symbol_z, table_x, table_y, table_z,
     out,
     space, mx, my, mz, sx, sy, sz, send_a, recv_a, send_b, recv_b, inverse,
-    b_send, b_recv, ready,
+    b_send, b_recv,
 ):
     fields, pack, rows, cols, cuts, xc, yb, zl = dims
     groups = fields // pack
@@ -118,7 +118,7 @@
     def batch_of(i):
         return [i in batch for batch in batches].index(True)
 
-    def first_part(load_sem, a_send, a_recv):
+    def first_part(load_sem, a_send, a_recv, ready):
         pieces = [(species.at[f], space.at[f]) for f in range(fields)]
         pieces += [(table_x.at[q], mx.at[q]) for q in range(cuts)]
         pieces += [(symbol_x, sx), (symbol_y, sy), (symbol_z, sz), (table_y, my), (table_z, mz)]
@@ -235,7 +235,7 @@
         pltpu.make_async_copy(sent, sent, a_send).wait()
 
     dma = pltpu.SemaphoreType.DMA
-    pl.run_scoped(first_part, dma((fields + cuts + 5,)), dma, dma((len(chunks),)))
+    pl.run_scoped(first_part, dma((fields + cuts + 5,)), dma, dma((len(chunks),)), pltpu.SemaphoreType.REGULAR)
 
     height = xc * yb
     for batch in batches:
@@ -309,7 +309,6 @@
             pltpu.VMEM((xb, yb, z), jnp.float32),
             dma,
             dma((len(batch_list(chunks)),)),
-            pltpu.SemaphoreType.REGULAR,
         ],
         compiler_params=pltpu.CompilerParams(
             collective_id=0, has_side_effects=True, vmem_limit_bytes=60 * 1024 * 1024

time: 15.4 us -> 15.4 us (level)
  no operation moved by 1% of the time
where the time goes in v4:
time: 15.4 us; the launch traced here: 15.2 us
  Pallas kernels  14.5 us (94%)
  local copies, waits for them, and re-layouts  0.71 us (5%)
    pallas_call x1, Pallas kernels, on_device(): pl.pallas_call(functools.partial(kernel, (fields, pack, rows, cols, cuts,...  14.5 us
    unnamed x1, local copies, waits for them, and re-layouts  0.71 us

profile of v4, /device:TPU:0, one launch (start us, length us, event | category | flops | bytes accessed | tf_op | source)
XLA Modules:
  0.0 15.2 jit_solution(15450833614944390925)
XLA Ops:
  0.0 14.5 %shard_map.73 = f32[4,64,256]{2,1,0:T(8,128)S(1)} custom-call(f32[4,256,64]{2,1,0:T(8,128)} %bitcast.4, f32[64]{0:T(128)} %symbol_x.1, f32[32]{0:T(128)} %symbol_y.1, f32[1,256]{1,0:T(1,128)} %bitcast.5, bf16[4,128,256]{2,1,0:T(8,128)(2,1)} %constant.6.clone.table_x, bf16[128,64]{1,0:T(8,128)(2,1)} %constant.7.clone.table_y, ...), custom_call_target="tpu_custom_call" | custom-call | tf_op jit(solution)/shard_map/pallas_call | solution.py:292
  14.5 0.7 %copy.9 = f32[4,8,8,256]{3,2,1,0:T(8,128)} copy(f32[4,8,8,256]{3,2,1,0:T(8,128)S(1)} %bitcast.3) | data formatting | bytes 524288

commit v5 on v3

--- a/solution.py
+++ b/solution.py
@@ -11,7 +11,7 @@
 
 MESH = pl.DeviceIdType.MESH
 LANES = 128
-PIECES = 4
+PIECES = 8
 SUBLANES = 8
 
 

time: 15.4 us -> 15.4 us (level)
  no operation moved by 1% of the time
where the time goes in v5:
time: 15.4 us; the launch traced here: 15.3 us
  Pallas kernels  14.5 us (94%)
  local copies, waits for them, and re-layouts  0.71 us (5%)
    pallas_call x1, Pallas kernels, on_device(): pl.pallas_call(functools.partial(kernel, (fields, pack, rows, cols, cuts,...  14.5 us
    unnamed x1, local copies, waits for them, and re-layouts  0.71 us

profile of v5, /device:TPU:0, one launch (start us, length us, event | category | flops | bytes accessed | tf_op | source)
XLA Modules:
  0.0 15.3 jit_solution(4993404456347975131)
XLA Ops:
  0.0 14.5 %shard_map.73 = f32[4,64,256]{2,1,0:T(8,128)S(1)} custom-call(f32[4,256,64]{2,1,0:T(8,128)} %bitcast.4, f32[64]{0:T(128)} %symbol_x.1, f32[32]{0:T(128)} %symbol_y.1, f32[1,256]{1,0:T(1,128)} %bitcast.5, bf16[4,128,256]{2,1,0:T(8,128)(2,1)} %constant.6.clone.table_x, bf16[128,64]{1,0:T(8,128)(2,1)} %constant.7.clone.table_y, ...), custom_call_target="tpu_custom_call" | custom-call | tf_op jit(solution)/shard_map/pallas_call | solution.py:292
  14.6 0.7 %copy.9 = f32[4,8,8,256]{3,2,1,0:T(8,128)} copy(f32[4,8,8,256]{3,2,1,0:T(8,128)S(1)} %bitcast.3) | data formatting | bytes 524288
